TPU v7x, 16 devices: a whole 2x2x2 slice. The times are simulated.
16 devices in a mesh: ez: 2 (over z), ey: 2 (over y), ex: 4 (over x, core).
Axes of the slice: x: 2, y: 2, z: 2, core: 2. Of those that a mesh axis runs over, the one named last changes fastest.
Arguments:
- x_tokens: bfloat16 [8192, 2048], P(('ez', 'ey', 'ex'))
- expert_ids: int32 [8192, 6], P(('ez', 'ey', 'ex'))
- gate_vals: float32 [8192, 6], P(('ez', 'ey', 'ex'))
- w_gate: bfloat16 [64, 2048, 1408], P(('ex', 'ey', 'ez'))
- w_up: bfloat16 [64, 2048, 1408], P(('ex', 'ey', 'ez'))
- w_down: bfloat16 [64, 1408, 2048], P(('ex', 'ey', 'ez'))
Outputs:
- output: bfloat16 [8192, 2048], P(('ez', 'ey', 'ex'))
All inputs are finite; a program needn't handle non-finite values.
Results may differ from a plain program's by a relative error of at most 0.00115.
Values are sent between devices in bfloat16 or wider.
A program may use at most 1 GiB of HBM per device.

v0:
```python
import jax
import jax.numpy as jnp
from jax import lax
from jax.sharding import PartitionSpec as P

TOKEN_AXES = ('ez', 'ey', 'ex')
EXPERT_AXES = ('ex', 'ey', 'ez')


def slot_layout(ids_local, n_exp, cap_slot):
    tok_dev, top_k = ids_local.shape
    flat_ids = ids_local.reshape(-1)
    match_mat = (flat_ids[:, None] == jnp.arange(n_exp)[None, :]).astype(jnp.int32)
    slot_rank = jnp.sum(jnp.cumsum(match_mat, axis=0) * match_mat, axis=1) - 1
    slot_idx = flat_ids * cap_slot + slot_rank
    pair_tok = jnp.arange(tok_dev * top_k, dtype=jnp.int32) // top_k
    slot_tok = jnp.zeros((n_exp * cap_slot,), jnp.int32).at[slot_idx].set(pair_tok)
    return slot_idx, slot_tok


def solution(mesh):
    n_dev = mesh.shape['ez'] * mesh.shape['ey'] * mesh.shape['ex']

    def local_layer(x_loc, ids_loc, gates_loc, w_g, w_u, w_d):
        tok_dev, hid_dim = x_loc.shape
        top_k = ids_loc.shape[1]
        n_local = w_g.shape[0]
        n_exp = n_local * n_dev
        cap_slot = 2 * tok_dev * top_k // n_exp
        slot_idx, slot_tok = slot_layout(ids_loc, n_exp, cap_slot)
        send_buf = jnp.take(x_loc, slot_tok, axis=0).reshape(n_dev, n_local, cap_slot, hid_dim)
        recv_buf = lax.all_to_all(send_buf, EXPERT_AXES, 0, 0)
        h_gate = jnp.einsum('slch,lhf->slcf', recv_buf, w_g, preferred_element_type=jnp.float32)
        h_up = jnp.einsum('slch,lhf->slcf', recv_buf, w_u, preferred_element_type=jnp.float32)
        act_bf = (jax.nn.silu(h_gate) * h_up).astype(jnp.bfloat16)
        exp_out = jnp.einsum('slcf,lfh->slch', act_bf, w_d, preferred_element_type=jnp.float32).astype(jnp.bfloat16)
        back_buf = lax.all_to_all(exp_out, EXPERT_AXES, 0, 0)
        back_flat = back_buf.reshape(n_exp * cap_slot, hid_dim)
        tok_rows = jnp.take(back_flat, slot_idx, axis=0).reshape(tok_dev, top_k, hid_dim)
        moe_sum = jnp.sum(gates_loc[:, :, None] * tok_rows, axis=1)
        return (x_loc.astype(jnp.float32) + moe_sum).astype(jnp.bfloat16)

    tok_spec = P(TOKEN_AXES, None)
    w_spec = P(EXPERT_AXES, None, None)
    return jax.shard_map(local_layer, mesh=mesh, in_specs=(tok_spec, tok_spec, tok_spec, w_spec, w_spec, w_spec), out_specs=tok_spec, check_vma=False)
```

profile of v0, /device:TPU:5, one launch (start us, length us, event | category | flops | bytes accessed | tf_op | source)
XLA Modules:
  0.0 1016.5 jit_solution(15222112656059123717)
XLA Ops:
  0.0 1.0 copy.28
  1.4 0.7 broadcast_multiply_fusion
  2.1 0.9 fusion.18
  3.0 31.9 %reduce-window.6 = s32[64,24,128]{2,1,0:T(8,128)S(1)} reduce-window(s32[64,24,128]{2,1,0:T(8,128)} %fusion.18, s32[]{:T(128)} %constant.32.clone.1), window={size=1x1x128 pad=0_0x0_0x127_0}, to_apply=%region_0.0 | reduce-window | flops 24969216 | bytes 1572868 | tf_op jit(solution)/shard_map/reduce-window
  34.9 1.2 slice.12
  36.1 1.6 copy.41
  37.6 0.2 reduce-window.9
  37.8 0.3 broadcast_add_fusion
  38.7 0.6 copy-done.5
  39.3 11.8 %scatter_custom_fusion = s32[6144]{0:T(1024)S(1)} fusion(s32[3072]{0:T(1024)S(1)} %bitcast.64, s32[3072]{0:T(1024)S(1)} %add_select_fusion, s32[]{:T(128)} %constant.32.clone.1), kind=kCustom, calls=%fused_computation.41 | custom fusion | bytes 24580 | tf_op jit(solution)/shard_map/scatter | solution.py:17
  51.2 30.9 %gather_fusion = bf16[6144,2048]{1,0:T(8,128)(2,1)} fusion(bf16[512,2048]{1,0:T(8,128)(2,1)S(1)} %copy-done, s32[6144]{0:T(1024)S(1)} %fusion.19), kind=kCustom, calls=%fused_computation | custom fusion | bytes 50356224 | tf_op jit(solution)/shard_map/jit(_take)/gather | solution.py:31
  82.2 12.5 %broadcast_select_fusion = bf16[16,4,96,2048]{3,2,1,0:T(8,128)(2,1)S(1)} fusion(bf16[16,4,96,2048]{3,2,1,0:T(8,128)(2,1)} %bitcast.59, pred[16,4,96]{2,1,0:T(4,128)(4,1)S(1)} %broadcast_in_dim.32), kind=kLoop, calls=%fused_computation.12 | loop fusion | flops 12582912 | bytes 50337792 | tf_op jit(solution)/shard_map/jit(_take)/select_n | solution.py:31
  94.7 284.8 %all_to_all.10 = bf16[16,4,96,2048]{3,2,1,0:T(8,128)(2,1)} all-to-all(bf16[16,4,96,2048]{3,2,1,0:T(8,128)(2,1)S(1)} %broadcast_select_fusion), channel_id=1, replica_groups=mesh['ez'=2,'ey'=2,'ex'=4] {'ex','ey','ez'}, dimensions={0} | all-to-all | bytes 50331648 | tf_op jit(solution)/shard_map/all_to_all | solution.py:32
  379.5 47.8 %fusion.10 = f32[4,16,96,1408]{3,2,1,0:T(8,128)} fusion(bf16[4,2048,1408]{2,1,0:T(8,128)(2,1)} %param.9, bf16[16,4,96,2048]{3,2,1,0:T(8,128)(2,1)} %all_to_all.10), kind=kOutput, calls=%fused_computation.17 | convolution fusion | flops 35433480192 | bytes 82837504 | tf_op jit(solution)/shard_map/slch,lhf->slcf/dot_general | solution.py:33
  427.3 51.9 %fusion = bf16[16,4,96,1408]{3,2,0,1:T(8,128)(2,1)} fusion(f32[4,16,96,1408]{3,2,1,0:T(8,128)} %fusion.10, bf16[4,2048,1408]{2,1,0:T(8,128)(2,1)} %param.10, bf16[16,4,96,2048]{3,2,1,0:T(8,128)(2,1)} %all_to_all.10), kind=kOutput, calls=%fused_computation.4 | convolution fusion | flops 35485384704 | bytes 100139008 | tf_op jit(solution)/shard_map/slch,lhf->slcf/dot_general | solution.py:34
  479.2 47.8 %convert_bitcast_fusion = bf16[16,4,96,2048]{3,2,0,1:T(8,128)(2,1)} fusion(bf16[16,4,96,1408]{3,2,0,1:T(8,128)(2,1)} %fusion, bf16[4,1408,2048]{2,1,0:T(8,128)(2,1)} %param.11), kind=kOutput, calls=%fused_computation.11 | convolution fusion | flops 35446063104 | bytes 65536000 | tf_op jit(solution)/shard_map/slcf,lfh->slch/dot_general | solution.py:36
  527.0 21.0 %copy.37 = bf16[16,4,96,2048]{3,2,1,0:T(8,128)(2,1)} copy(bf16[16,4,96,2048]{3,2,0,1:T(8,128)(2,1)} %convert_bitcast_fusion) | data formatting | bytes 50331648 | tf_op jit(solution)/shard_map/convert_element_type | solution.py:36
  548.1 4.6 all-to-all-start.1
  552.7 0.2 sub.15
  553.4 385.9 %all-to-all-done.1 = bf16[16,4,96,2048]{3,2,1,0:T(8,128)(2,1)} async-done(((bf16[16,4,96,2048]{3,2,1,0:T(8,128)(2,1)}), bf16[16,4,96,2048]{3,2,1,0:T(8,128)(2,1)}, u32[]{:S(2)}, u32[]{:S(2)}) %all-to-all-start.1) | async-done | bytes 25165856 | tf_op jit(solution)/shard_map/all_to_all | solution.py:37
  939.3 35.2 %gather_fusion.1 = bf16[3072,2048]{1,0:T(8,128)(2,1)} fusion(bf16[6144,2048]{1,0:T(8,128)(2,1)} %bitcast.15, s32[3072]{0:T(1024)S(1)} %broadcast_clamp_fusion), kind=kCustom, calls=%fused_computation.1 | custom fusion | bytes 25178112 | tf_op jit(solution)/shard_map/jit(_take)/gather | solution.py:39
  974.5 20.5 %gather.15 = bf16[512,6,2048]{2,1,0:T(8,128)(2,1)} reshape(bf16[3072,2048]{1,0:T(8,128)(2,1)} %gather_fusion.1) | data formatting | bytes 25165824 | tf_op jit(solution)/shard_map/jit(_take)/gather | solution.py:39
  995.0 19.4 %multiply_reduce_fusion = f32[512,2048]{1,0:T(8,128)S(1)} fusion(bf16[512,6,2048]{2,1,0:T(8,128)(2,1)} %gather.15, f32[512,6]{1,0:T(8,128)S(1)} %copy.27, pred[512,6]{1,0:T(8,128)(4,1)S(1)} %copy.33), kind=kLoop, calls=%fused_computation.10 | loop fusion | flops 24117248 | bytes 16792576 | tf_op jit(solution)/shard_map/reduce_sum | solution.py:40
  1014.4 2.1 add_convert_fusion
  (31 shorter events, 1.5 us)
Async XLA Ops:
  0.0 51.2 %copy-start = (bf16[512,2048]{1,0:T(8,128)(2,1)S(1)}, bf16[512,2048]{1,0:T(8,128)(2,1)}, u32[]{:S(2)}) copy-start(bf16[512,2048]{1,0:T(8,128)(2,1)} %param.6) | copy-start | bytes 6291460
  38.3 43.9 %copy-start.3 = (s32[3072]{0:T(1024)}, s32[3072]{0:T(1024)S(1)}, u32[]{:S(2)}) copy-start(s32[3072]{0:T(1024)S(1)} %broadcast_add_fusion.1) | copy-start | bytes 36868
  38.7 0.6 copy-start.5
  548.0 4.6 copy-start.4
  548.1 4.9 copy-start.2
  548.1 5.2 copy-start.7
  548.1 5.3 copy-start.6
  548.1 391.2 %all-to-all-start.1 = ((bf16[16,4,96,2048]{3,2,1,0:T(8,128)(2,1)}), bf16[16,4,96,2048]{3,2,1,0:T(8,128)(2,1)}, u32[]{:S(2)}, u32[]{:S(2)}) async-start(bf16[16,4,96,2048]{3,2,1,0:T(8,128)(2,1)} %copy.37), calls=%async_computation.1 | async-start | bytes 50331648 | tf_op jit(solution)/shard_map/all_to_all | solution.py:37
  974.5 39.9 %copy-start.1 = (bf16[512,2048]{1,0:T(8,128)(2,1)S(1)}, bf16[512,2048]{1,0:T(8,128)(2,1)}, u32[]{:S(2)}) copy-start(bf16[512,2048]{1,0:T(8,128)(2,1)} %param.6) | copy-start | bytes 6291460
where the time goes:
time: 1020 us
  waiting for transfers between devices  386 us (38%)
  blocking collectives  285 us (28%)
  matrix products  147 us (14%)
  local copies, waits for them, and re-layouts  125 us (12%)
  other arithmetic  68.3 us (7%)
    all_to_all x1, waiting for transfers between devices, local_layer(): back_buf = lax.all_to_all(exp_out, EXPERT_AXES, 0, 0)  386 us
    all_to_all x1, blocking collectives, local_layer(): recv_buf = lax.all_to_all(send_buf, EXPERT_AXES, 0, 0)  285 us
    gather x2, local copies, waits for them, and re-layouts, local_layer(): jnp.take(back_flat, slot_idx, axis=0).reshape(tok_dev, top_k, hid_dim)  55.7 us
    dot_general x1, matrix products, local_layer(): jnp.einsum('slch,lhf->slcf', recv_buf, w_u, preferred_element_type=jnp.fl...  51.9 us
    dot_general x1, matrix products, local_layer(): jnp.einsum('slch,lhf->slcf', recv_buf, w_g, preferred_element_type=jnp.fl...  47.8 us
    dot_general x1, matrix products, local_layer(): jnp.einsum('slcf,lfh->slch', act_bf, w_d, preferred_element_type=jnp.floa...  47.8 us
    another operation x3, other arithmetic  32.4 us
    gather x1, local copies, waits for them, and re-layouts, local_layer(): jnp.take(x_loc, slot_tok, axis=0).reshape(n_dev, n_local, cap_slot, hid_dim)  30.9 us
  transfers between devices with their start and end apart: 1, of which 1 were waited for; matrix products, arithmetic and copies ran while one was open for 0% of the time, Pallas kernels for 0%

commit v1 on v0

v1 whole, which is shorter than its diff:
```python
import jax
import jax.numpy as jnp
from jax import lax
from jax.sharding import PartitionSpec as P

TOKEN_AXES = ('ez', 'ey', 'ex')
EXPERT_AXES = ('ex', 'ey', 'ez')


def routing(ids, gates, n_exp):
    tok_dev = ids.shape[0]
    hit = ids[:, :, None] == jnp.arange(n_exp)[None, None, :]
    picked = jnp.any(hit, axis=1)
    gate = jnp.sum(jnp.where(hit, gates[:, :, None], 0.0), axis=1)
    below = (jnp.arange(tok_dev)[:, None] > jnp.arange(tok_dev)[None, :]).astype(jnp.bfloat16)
    rank = jnp.dot(below, picked.astype(jnp.bfloat16), preferred_element_type=jnp.float32)
    return hit, picked, rank, gate


def solution(mesh):
    n_dev = mesh.shape['ez'] * mesh.shape['ey'] * mesh.shape['ex']

    def local_layer(x_loc, ids_loc, gates_loc, w_g, w_u, w_d):
        tok_dev, hid = x_loc.shape
        top_k = ids_loc.shape[1]
        n_local = w_g.shape[0]
        n_exp = n_local * n_dev
        cap = 2 * tok_dev * top_k // n_exp
        x_all = lax.all_gather(x_loc, TOKEN_AXES, tiled=True)
        hit, picked, rank, gate = routing(ids_loc, gates_loc, n_exp)
        code = jnp.where(picked, rank, -1.0).T.reshape(n_dev, n_local, tok_dev)
        code = lax.all_to_all(code, EXPERT_AXES, 0, 0)
        slot = jnp.arange(cap, dtype=jnp.float32)
        match = code[:, :, None, :] == slot[None, None, :, None]
        slot_tok = jnp.sum(jnp.where(match, jnp.arange(tok_dev, dtype=jnp.int32), 0), axis=-1)
        nz, ny, nx = mesh.shape['ez'], mesh.shape['ey'], mesh.shape['ex']
        num = jnp.arange(n_dev)
        tok_num = ((num % nz) * ny + (num // nz) % ny) * nx + num // (nz * ny)
        rows = (tok_num[:, None, None] * tok_dev + slot_tok)
        rows = rows.transpose(1, 0, 2).reshape(-1)
        xs = jnp.take(x_all, rows, axis=0, mode='clip').reshape(n_local, n_dev * cap, hid)
        h_gate = jnp.einsum('lch,lhf->lcf', xs, w_g, preferred_element_type=jnp.float32)
        h_up = jnp.einsum('lch,lhf->lcf', xs, w_u, preferred_element_type=jnp.float32)
        act = (jax.nn.silu(h_gate) * h_up).astype(jnp.bfloat16)
        out = jnp.einsum('lcf,lfh->lch', act, w_d, preferred_element_type=jnp.float32).astype(jnp.bfloat16)
        out = out.reshape(n_local, n_dev, cap, hid)
        back = lax.all_to_all(out, EXPERT_AXES, 1, 1)
        back = back.reshape(n_local * n_dev * cap, hid)
        rank_j = jnp.sum(jnp.where(hit, rank[:, None, :], 0.0), axis=-1).astype(jnp.int32)
        slot_idx = ((ids_loc % n_local) * n_dev + ids_loc // n_local) * cap + rank_j
        acc = x_loc.astype(jnp.float32)
        tok_rows = jnp.take(back, slot_idx.reshape(-1), axis=0, mode='clip').reshape(tok_dev, top_k, hid)
        acc = acc + jnp.sum(gates_loc[:, :, None] * tok_rows, axis=1)
        return acc.astype(jnp.bfloat16)

    tok = P(TOKEN_AXES, None)
    w = P(EXPERT_AXES, None, None)
    return jax.shard_map(local_layer, mesh=mesh, in_specs=(tok, tok, tok, w, w, w), out_specs=tok, check_vma=False)
```

time: 1020 us -> 1040 us (1.020)
  blocking collectives: 285 us -> 0 us
  local copies, waits for them, and re-layouts: 125 us -> 327 us
  waiting for transfers between devices: 386 us -> 514 us
  other arithmetic: 68.3 us -> 22 us
  between operations: 0.21 us -> 13.5 us
    all_to_all x1 -> x0, blocking collectives: 285 us -> none  [local_layer(): recv_buf = lax.all_to_all(send_buf, EXPERT_AXES, 0, 0)]
    gather x3 -> x2, local copies, waits for them, and re-layouts: 86.7 us -> 260 us  [the longest x1 225 us: local_layer(): jnp.take(x_all, rows, axis=0, mode='clip')]
    all_gather x0 -> x1, waiting for transfers between devices: none -> 122 us  [local_layer(): x_all = lax.all_gather(x_loc, TOKEN_AXES, tiled=True)]
    another operation x3 -> x0, other arithmetic: 32.4 us -> none
    reshape x1 -> x2, local copies, waits for them, and re-layouts: 0.17 us -> 21.8 us  [the longest x1 21.1 us: local_layer(): out = out.reshape(n_local, n_dev, cap, hid)]
    all_to_all x0 -> x1, local copies, waits for them, and re-layouts: none -> 21.1 us  [local_layer(): back = lax.all_to_all(out, EXPERT_AXES, 1, 1)]
    select_n x3 -> x1, other arithmetic: 12.6 us -> 0.02 us  [local_layer(): code = jnp.where(picked, rank, -1.0).T.reshape(n_dev, n_local, tok_dev)]
    scatter x1 -> x0, local copies, waits for them, and re-layouts: 11.8 us -> none  [slot_layout(): jnp.zeros((n_exp * cap_slot,), jnp.int32).at[slot_idx].set(pair_tok)]
  transfers between devices with their start and end apart: 1 -> 3, of which waited for: 1 -> 3; matrix products, arithmetic and copies ran while one was open for 0% -> 0% of each run, Pallas kernels for 0% -> 0%
where the time goes in v1:
time: 1040 us
  waiting for transfers between devices  514 us (49%)
  local copies, waits for them, and re-layouts  327 us (31%)
  matrix products  149 us (14%)
  other arithmetic  22 us (2%)
  starting transfers between devices  13.7 us (1%)
  between operations  13.5 us (1%)
    all_to_all x1, waiting for transfers between devices, local_layer(): back = lax.all_to_all(out, EXPERT_AXES, 1, 1)  387 us
    gather x1, local copies, waits for them, and re-layouts, local_layer(): jnp.take(x_all, rows, axis=0, mode='clip')  225 us
    all_gather x1, waiting for transfers between devices, local_layer(): x_all = lax.all_gather(x_loc, TOKEN_AXES, tiled=True)  122 us
    dot_general x1, matrix products, local_layer(): jnp.einsum('lch,lhf->lcf', xs, w_u, preferred_element_type=jnp.float32)  53 us
    dot_general x1, matrix products, local_layer(): jnp.einsum('lch,lhf->lcf', xs, w_g, preferred_element_type=jnp.float32)  47.8 us
    dot_general x1, matrix products, local_layer(): jnp.einsum('lcf,lfh->lch', act, w_d, preferred_element_type=jnp.float32)  47.7 us
    gather x1, local copies, waits for them, and re-layouts, local_layer(): jnp.take(back, slot_idx.reshape(-1), axis=0, mode='clip')  35.2 us
    convert_element_type x1, local copies, waits for them, and re-layouts, local_layer(): acc = acc + jnp.sum(gates_loc[:, :, None] * tok_rows, axis=1)  22.2 us
  transfers between devices with their start and end apart: 3, of which 3 were waited for; matrix products, arithmetic and copies ran while one was open for 0% of the time, Pallas kernels for 0%

profile of v1, /device:TPU:5, one launch (start us, length us, event | category | flops | bytes accessed | tf_op | source)
XLA Modules:
  0.0 1039.0 jit_solution(11859254337959680561)
XLA Ops:
  6.5 0.7 all-gather.2.cloned.1.call-update
  7.3 0.8 fusion.2
  8.1 0.3 fusion.1
  8.4 0.7 copy-done.1
  9.0 0.7 reshape.68
  9.7 4.3 all-to-all-start
  14.0 4.5 all-to-all-done
  18.5 1.4 select_reduce_fusion
  20.2 122.1 %all-gather.2.cloned.1.call-done = bf16[8192,2048]{1,0:T(8,128)(2,1)} async-done(((bf16[512,2048]{1,0:T(8,128)(2,1)}), bf16[8192,2048]{1,0:T(8,128)(2,1)}) %all-gather.2.cloned.1.call-update) | async-done | bytes 33554448 | tf_op jit(solution)/shard_map/all_gather | solution.py:29
  142.3 225.2 %gather_fusion = bf16[6144,2048]{1,0:T(8,128)(2,1)} fusion(bf16[8192,2048]{1,0:T(8,128)(2,1)} %all-gather.2.cloned.1.call-done, s32[6144]{0:T(1024)S(1)} %broadcast_clamp_fusion), kind=kCustom, calls=%fused_computation | custom fusion | bytes 50356224 | tf_op jit(solution)/shard_map/jit(_take)/gather | solution.py:41
  367.5 47.8 %fusion.17 = f32[4,1536,1408]{2,1,0:T(8,128)} fusion(bf16[4,1536,2048]{2,1,0:T(8,128)(2,1)} %bitcast.16, bf16[4,2048,1408]{2,1,0:T(8,128)(2,1)} %param.9), kind=kOutput, calls=%fused_computation.49 | convolution fusion | flops 35433480192 | bytes 82837504 | tf_op jit(solution)/shard_map/lch,lhf->lcf/dot_general | solution.py:42
  415.3 53.0 %fusion = bf16[4,1536,1408]{2,1,0:T(8,128)(2,1)} fusion(bf16[4,1536,2048]{2,1,0:T(8,128)(2,1)} %bitcast.17, bf16[4,2048,1408]{2,1,0:T(8,128)(2,1)} %param.10, f32[4,1536,1408]{2,1,0:T(8,128)} %fusion.17), kind=kOutput, calls=%fused_computation.5 | convolution fusion | flops 35485384704 | bytes 100139008 | tf_op jit(solution)/shard_map/lch,lhf->lcf/dot_general | solution.py:43
  468.3 47.7 %convolution_convert_fusion = bf16[4,1536,2048]{2,1,0:T(8,128)(2,1)} fusion(bf16[4,1536,1408]{2,1,0:T(8,128)(2,1)} %fusion, bf16[4,1408,2048]{2,1,0:T(8,128)(2,1)} %param.11), kind=kOutput, calls=%fused_computation.4 | convolution fusion | flops 35446063104 | bytes 65536000 | tf_op jit(solution)/shard_map/lcf,lfh->lch/dot_general | solution.py:45
  516.0 21.1 %copy.22 = bf16[4,16,96,2048]{3,2,0,1:T(8,128)(2,1)} copy(bf16[4,16,96,2048]{3,2,1,0:T(8,128)(2,1)} %bitcast.15) | data formatting | bytes 50331648 | tf_op jit(solution)/shard_map/reshape | solution.py:46
  537.1 9.5 all-to-all-start.1
  546.7 0.1 copy.24
  546.9 0.2 reshape.83
  547.1 0.1 copy.20
  547.2 387.0 %all-to-all-done.1 = bf16[4,16,96,2048]{3,2,0,1:T(8,128)(2,1)} async-done(((bf16[4,16,96,2048]{3,2,0,1:T(8,128)(2,1)}), bf16[4,16,96,2048]{3,2,0,1:T(8,128)(2,1)}, u32[]{:S(2)}, u32[]{:S(2)}) %all-to-all-start.1) | async-done | bytes 25165856 | tf_op jit(solution)/shard_map/all_to_all | solution.py:47
  934.2 21.1 %copy.23 = bf16[4,16,96,2048]{3,2,1,0:T(8,128)(2,1)} copy(bf16[4,16,96,2048]{3,2,0,1:T(8,128)(2,1)} %all-to-all-done.1) | data formatting | bytes 50331648 | tf_op jit(solution)/shard_map/all_to_all | solution.py:47
  955.3 35.2 %gather_fusion.1 = bf16[3072,2048]{1,0:T(8,128)(2,1)} fusion(bf16[6144,2048]{1,0:T(8,128)(2,1)} %bitcast.14, s32[3072]{0:T(1024)S(1)} %broadcast_clamp_fusion.1), kind=kCustom, calls=%fused_computation.1 | custom fusion | bytes 25178112 | tf_op jit(solution)/shard_map/jit(_take)/gather | solution.py:52
  990.5 22.2 %reshape.72 = f32[512,6,2048]{2,1,0:T(8,128)} reshape(bf16[3072,2048]{1,0:T(8,128)(2,1)} %gather_fusion.1) | data formatting | bytes 37748736 | tf_op jit(solution)/shard_map/convert_element_type | solution.py:53
  1012.7 17.4 %multiply_reduce_fusion = f32[512,2048]{1,0:T(8,128)S(1)} fusion(f32[512,6,2048]{2,1,0:T(8,128)} %reshape.72, f32[512,6]{1,0:T(8,128)S(1)} %copy.20), kind=kLoop, calls=%fused_computation.3 | loop fusion | flops 11534336 | bytes 29372416 | tf_op jit(solution)/shard_map/reduce_sum | solution.py:53
  1030.1 2.1 add_convert_fusion
  (19 shorter events, 0.3 us)
Async XLA Ops:
  6.5 135.8 %all-gather.2.cloned.1.call-start = ((), (), s32[]{:S(2)}) async-start(), calls=%async_computation.2 | async-start | bytes 35651584 | tf_op jit(solution)/shard_map/all_gather | solution.py:29
  8.4 0.7 copy-start.1
  9.7 8.8 all-to-all-start
  537.1 9.5 copy-start.2
  537.1 9.5 copy-start.3
  537.1 10.0 copy-start.4
  537.1 397.1 %all-to-all-start.1 = ((bf16[4,16,96,2048]{3,2,0,1:T(8,128)(2,1)}), bf16[4,16,96,2048]{3,2,0,1:T(8,128)(2,1)}, u32[]{:S(2)}, u32[]{:S(2)}) async-start(bf16[4,16,96,2048]{3,2,0,1:T(8,128)(2,1)} %copy.22), calls=%async_computation.1 | async-start | bytes 50331648 | tf_op jit(solution)/shard_map/all_to_all | solution.py:47
  1012.7 17.4 %copy-start = (bf16[512,2048]{1,0:T(8,128)(2,1)S(1)}, bf16[512,2048]{1,0:T(8,128)(2,1)}, u32[]{:S(2)}) copy-start(bf16[512,2048]{1,0:T(8,128)(2,1)} %param.6) | copy-start | bytes 6291460
Sparse Core Ops, SparseCore 0:
  9.6 132.7 all-gather.1

commit v2 on v0

v2 whole, which is shorter than its diff:
```python
import functools

import jax
import jax.numpy as jnp
from jax import lax
from jax.experimental import pallas as pl
from jax.experimental.pallas import tpu as pltpu
from jax.sharding import PartitionSpec as P

TOKEN_AXES = ('ez', 'ey', 'ex')
EXPERT_AXES = ('ex', 'ey', 'ez')
MESH = pl.DeviceIdType.MESH
BF16, F32 = jnp.bfloat16, jnp.float32

N_DEV = 16
N_LOC = 4
N_EXP = N_DEV * N_LOC
TOK = 512
HID = 2048
FFN = 1408
CAP = 96
RET = 240
SLOTS = N_LOC * CAP
UNITS = (1, 3, 3, 1)
FIRST = (0, 1, 4, 7)


def routing(ids, gates):
    hit = ids[:, :, None] == jnp.arange(N_EXP)[None, None, :]
    picked = jnp.any(hit, axis=1)
    gate = jnp.sum(jnp.where(hit, gates[:, :, None], 0.0), axis=1)
    below = (jnp.arange(TOK)[:, None] > jnp.arange(TOK)[None, :]).astype(BF16)
    rank = jnp.dot(below, picked.astype(BF16), preferred_element_type=F32)
    return hit, picked, rank, gate


def tables(ids, gates):
    hit, picked, rank, gate = routing(ids, gates)
    cnt = jnp.sum(picked.astype(F32), axis=0).reshape(N_DEV, N_LOC)
    tri = (jnp.arange(N_LOC)[:, None] > jnp.arange(N_LOC)[None, :]).astype(F32)
    off = jnp.sum(cnt[:, None, :] * tri[None], axis=-1)
    over = jnp.max(jnp.sum(cnt, axis=1)) > RET
    code = jnp.where(picked, rank, -1.0).T.reshape(N_DEV, N_LOC, TOK)
    slot = jnp.arange(CAP, dtype=F32)
    pos = jnp.where(slot < cnt[:, :, None], off[:, :, None] + slot, -1.0).reshape(N_DEV, 1, SLOTS)
    pos = jnp.pad(pos, ((0, 0), (0, 0), (0, TOK - SLOTS)), constant_values=-1.0)
    flag = jnp.broadcast_to(over.astype(F32), (N_DEV, 3, TOK))
    codes = jnp.concatenate([code, pos, flag], axis=1)
    place = jnp.where(picked, off.reshape(-1)[None] + rank, -1.0)
    comb = jnp.concatenate([place, gate], axis=1)
    return codes, comb


def flips(q):
    ct, i = (q + 2) // 3, (q + 2) % 3
    w1, w2, w3 = (ct % 2) * (1 - ct // 2), (1 - ct % 2) * (ct // 2), (ct % 2) * (ct // 2)
    base = ((3 - i) // 3, i % 2, i // 2)
    return tuple(w1 * f + w2 * (1 - f) + w3 for f in base)


def moe_kernel(x_ref, codes_ref, comb_ref, w1_ref, w3_ref, w2_ref,
               y_ref, flag_ref, x_all, h_send, h_recv,
               wb1, wb3, wb2, rows, act, xb, sb, meta, acc,
               w_sem, xl_sem, xs_sem, xr_sem, ms_sem, mr_sem, sl_sem, rs_sem, rr_sem, rl_sem):
    ez, ey, ex = (lax.axis_index(a) for a in TOKEN_AXES)
    core, xc = ex % 2, ex // 2
    my_tok = (ez * 2 + ey) * 4 + ex
    my_exp = (ex * 2 + ey) * 2 + ez

    def place(q, other):
        cs = core + other * (1 - 2 * core)
        fa, fb, fc = flips(q)
        fx = fa * (1 - cs) + fb * cs
        fy = fb * (1 - cs) + fc * cs
        fz = fc * (1 - cs) + fa * cs
        pz, py, px = ez + fz * (1 - 2 * ez), ey + fy * (1 - 2 * ey), xc + fx * (1 - 2 * xc)
        return pz, py, 2 * px + cs

    def tok_num(p):
        return (p[0] * 2 + p[1]) * 4 + p[2]

    def exp_num(p):
        return (p[2] * 2 + p[1]) * 2 + p[0]

    barrier = pltpu.get_barrier_semaphore()

    @pl.loop(1, N_DEV)
    def _(d):
        pl.semaphore_signal(barrier, inc=1, device_id=place(d // 2, d % 2), device_id_type=MESH)

    pl.semaphore_wait(barrier, N_DEV - 1)

    def x_copy(src, slot, n, dev):
        return pltpu.make_async_remote_copy(
            src_ref=src, dst_ref=x_all.at[slot], send_sem=xs_sem.at[n], recv_sem=xr_sem.at[slot],
            device_id=dev, device_id_type=MESH)

    sib = place(0, 1)
    nbr = {1: place(1, 0), 2: place(2, 0), 3: place(3, 0)}
    for n, q in enumerate((1, 2, 3)):
        x_copy(x_ref, q, n, nbr[q]).start()
    x_copy(x_ref, 8, 3, sib).start()

    def forward(q, via, to, n):
        x_copy(x_all.at[q], to, n, nbr[via]).start()

    def push(q):
        x_copy(x_all.at[q], 8 + q, 3 + q, sib).start()

    def arrived(slot):
        x_copy(x_ref, slot, 0, sib).wait_recv()

    def meta_copy(d):
        dev = place(d // 2, d % 2)
        return pltpu.make_async_remote_copy(
            src_ref=codes_ref.at[exp_num(dev)], dst_ref=meta.at[my_tok], send_sem=ms_sem.at[d],
            recv_sem=mr_sem.at[my_tok], device_id=dev, device_id_type=MESH)

    own_meta = pltpu.make_async_copy(codes_ref.at[my_exp], meta.at[my_tok], mr_sem.at[my_tok])
    own_meta.start()

    @pl.loop(1, N_DEV)
    def _(d):
        meta_copy(d).start()

    def meta_wait(num):
        pltpu.make_async_copy(codes_ref.at[0], meta.at[num], mr_sem.at[num]).wait()

    def w_copies(e, s):
        return [pltpu.make_async_copy(w.at[e], b.at[s], w_sem.at[s, k])
                for k, (w, b) in enumerate(((w1_ref, wb1), (w3_ref, wb3), (w2_ref, wb2)))]

    for c in w_copies(0, 0):
        c.start()

    def gather(ci):
        n, q0 = 2 * UNITS[ci], FIRST[ci]

        def load(d):
            slot = q0 + d // 2 + 8 * (d % 2)
            return pltpu.make_async_copy(x_all.at[slot], xb.at[d % 2], xl_sem.at[d % 2])

        def fetch(d):
            arrived(q0 + d // 2 + 8 * (d % 2))
            load(d).start()

        if ci == 0:
            pltpu.make_async_copy(x_ref, xb.at[0], xl_sem.at[0]).start()
        else:
            load(0).start()

        @pl.loop(0, n)
        def _(d):
            @pl.when(d + 1 < n)
            def _():
                if ci == 0:
                    fetch(d + 1)
                else:
                    @pl.when((d + 1) % 2 == 1)
                    def _():
                        arrived(q0 + (d + 1) // 2 + 8)
                    load(d + 1).start()
            dev = place(q0 + d // 2, d % 2)
            num = tok_num(dev)
            meta_wait(num)
            code = meta[num]
            want = lax.broadcasted_iota(jnp.int32, (CAP, TOK), 0).astype(F32)
            sel = jnp.concatenate(
                [jnp.where(code[e:e + 1, :] == want, 1.0, 0.0).astype(BF16) for e in range(N_LOC)], axis=0)
            load(d).wait()
            at = pl.multiple_of(d * CAP, CAP)

            @pl.loop(0, HID // 512)
            def _(t):
                cols = pl.ds(pl.multiple_of(t * 512, 512), 512)
                got = jnp.dot(sel, xb[d % 2, :, cols], preferred_element_type=F32).astype(BF16)
                for e in range(N_LOC):
                    rows[e, pl.ds(at, CAP), cols] = got[e * CAP:(e + 1) * CAP]

    def ffn(ci, e):
        m = UNITS[ci] * 2 * CAP
        s = e % 2
        for c in w_copies(e, s):
            c.wait()
        def prefetch():
            for c in w_copies((e + 1) % N_LOC, 1 - s):
                c.start()
        if ci < 3:
            prefetch()
        else:
            pl.when(e + 1 < N_LOC)(prefetch)

        @pl.loop(0, FFN // 128)
        def _(t):
            cols = pl.ds(pl.multiple_of(t * 128, 128), 128)
            w = jnp.concatenate([wb1[s, :, cols], wb3[s, :, cols]], axis=1)
            h = jnp.dot(rows[e, :m, :], w, preferred_element_type=F32)
            act[:m, cols] = (jax.nn.silu(h[:, :128]) * h[:, 128:]).astype(BF16)

        @pl.loop(0, HID // 512)
        def _(t):
            cols = pl.ds(pl.multiple_of(t * 512, 512), 512)
            rows[e, :m, cols] = jnp.dot(act[:m, :], wb2[s, :, cols], preferred_element_type=F32).astype(BF16)

    def ret_copy(d):
        dev = place(d // 2, d % 2)
        return pltpu.make_async_remote_copy(
            src_ref=h_send.at[d], dst_ref=h_recv.at[my_exp], send_sem=rs_sem.at[d],
            recv_sem=rr_sem.at[my_exp], device_id=dev, device_id_type=MESH)

    def stage(d):
        return pltpu.make_async_copy(sb.at[d % 2], h_send.at[d], sl_sem.at[d % 2])

    def send_back(ci):
        d0, n = 2 * FIRST[ci], 2 * UNITS[ci]

        @pl.loop(0, n)
        def _(k):
            d = d0 + k
            num = tok_num(place(d // 2, d % 2))
            pos = meta[num, 4:5, :SLOTS]
            want = lax.broadcasted_iota(jnp.int32, (RET, SLOTS), 0).astype(F32)
            sel = jnp.where(pos == want, 1.0, 0.0).astype(BF16)
            at = pl.multiple_of(k * CAP, CAP)

            @pl.loop(0, HID // 512)
            def _(t):
                cols = pl.ds(pl.multiple_of(t * 512, 512), 512)
                o = jnp.concatenate([rows[e, pl.ds(at, CAP), cols] for e in range(N_LOC)], axis=0)
                sb[d % 2, :, cols] = jnp.dot(sel, o, preferred_element_type=F32).astype(BF16)

            stage(d).start()

            @pl.when(k > 0)
            def _():
                stage(d - 1).wait()
                if ci == 0:
                    pass
                else:
                    ret_copy(d - 1).start()

        last = d0 + n - 1
        stage(last).wait()
        ret_copy(last).start()

    def experts(ci, between=None):
        @pl.loop(0, N_LOC)
        def _(e):
            ffn(ci, e)
            if between is not None:
                pl.when(e == 2)(between)

    gather(0)
    experts(0)
    send_back(0)
    for q in (1, 2, 3):
        arrived(q)
        if q == 1:
            forward(1, 3, 5, 11)
        elif q == 2:
            forward(2, 1, 6, 12)
        else:
            forward(3, 2, 4, 13)
    for q in (1, 2, 3):
        push(q)
    gather(1)

    def relay():
        arrived(4)
        forward(4, 1, 7, 14)
        push(4)
        for q in (5, 6):
            arrived(q)
            push(q)

    experts(1, relay)
    send_back(1)
    gather(2)

    def relay_last():
        arrived(7)
        push(7)

    experts(2, relay_last)
    send_back(2)
    gather(3)
    experts(3)
    send_back(3)

    acc[...] = x_to_f32(x_ref, xb, xl_sem, acc)

    def take(d):
        num = exp_num(place(d // 2, d % 2))
        return pltpu.make_async_copy(h_recv.at[num], sb.at[d % 2], rl_sem.at[d % 2])

    def came(d):
        num = exp_num(place(d // 2, d % 2))
        pltpu.make_async_remote_copy(
            src_ref=h_send.at[d], dst_ref=h_recv.at[num], send_sem=rs_sem.at[d],
            recv_sem=rr_sem.at[num], device_id=sib, device_id_type=MESH).wait_recv()

    pltpu.make_async_copy(h_send.at[0], sb.at[0], rl_sem.at[0]).start()

    @pl.loop(0, N_DEV)
    def _(d):
        @pl.when(d + 1 < N_DEV)
        def _():
            came(d + 1)
            take(d + 1).start()
        num = exp_num(place(d // 2, d % 2))
        tab = pltpu.roll(comb_ref[...], (2 * N_EXP - num * N_LOC) % (2 * N_EXP), 1)
        want = lax.broadcasted_iota(jnp.int32, (TOK, RET), 1).astype(F32)
        g = jnp.zeros((TOK, RET), F32)
        for e in range(N_LOC):
            g = jnp.where(tab[:, e:e + 1] == want, tab[:, N_EXP + e:N_EXP + e + 1], g)
        hi = g.astype(BF16)
        rest = g - hi.astype(F32)
        mid = rest.astype(BF16)
        lo = (rest - mid.astype(F32)).astype(BF16)
        lhs = jnp.concatenate([hi, mid, lo], axis=0)
        take(d).wait()

        @pl.loop(0, HID // 256)
        def _(t):
            cols = pl.ds(pl.multiple_of(t * 256, 256), 256)
            r = jnp.dot(lhs, sb[d % 2, :, cols], preferred_element_type=F32)
            acc[:, cols] += r[:TOK] + (r[TOK:2 * TOK] + r[2 * TOK:])

    y_ref[...] = acc[...].astype(BF16)
    flag_ref[...] = jnp.max(meta[:, 5:6, :128], axis=0) + jnp.zeros((8, 128), F32)

    for n in range(15):
        x_copy(x_ref, 0, n, sib).wait_send()

    @pl.loop(1, N_DEV)
    def _(d):
        meta_copy(d).wait_send()
        ret_copy(d).wait_send()


def x_to_f32(x_ref, xb, xl_sem, acc):
    c = pltpu.make_async_copy(x_ref, xb.at[0], xl_sem.at[0])
    c.start()
    c.wait()
    return xb[0].astype(F32)


def moe(x, codes, comb, w1, w3, w2):
    hbm = pl.BlockSpec(memory_space=pl.ANY)
    vmem = pl.BlockSpec(memory_space=pltpu.VMEM)
    dma = pltpu.SemaphoreType.DMA
    out = pl.pallas_call(
        moe_kernel,
        out_shape=(
            jax.ShapeDtypeStruct((TOK, HID), BF16),
            jax.ShapeDtypeStruct((8, 128), F32),
            jax.ShapeDtypeStruct((N_DEV, TOK, HID), BF16),
            jax.ShapeDtypeStruct((N_DEV, RET, HID), BF16),
            jax.ShapeDtypeStruct((N_DEV, RET, HID), BF16),
        ),
        in_specs=[hbm, hbm, vmem, hbm, hbm, hbm],
        out_specs=(vmem, vmem, hbm, hbm, hbm),
        scratch_shapes=[
            pltpu.VMEM((2, HID, FFN), BF16),
            pltpu.VMEM((2, HID, FFN), BF16),
            pltpu.VMEM((2, FFN, HID), BF16),
            pltpu.VMEM((N_LOC, 6 * CAP, HID), BF16),
            pltpu.VMEM((6 * CAP, FFN), BF16),
            pltpu.VMEM((2, TOK, HID), BF16),
            pltpu.VMEM((2, RET, HID), BF16),
            pltpu.VMEM((N_DEV, 8, TOK), F32),
            pltpu.VMEM((TOK, HID), F32),
            dma((2, 3)), dma((2,)), dma((15,)), dma((16,)), dma((16,)), dma((16,)),
            dma((2,)), dma((16,)), dma((16,)), dma((2,)),
        ],
        compiler_params=pltpu.CompilerParams(
            collective_id=0, has_side_effects=True, vmem_limit_bytes=67_043_328),
        name='moe',
    )(x, codes, comb, w1, w3, w2)
    return out[0], out[1]


def plain(x_loc, ids, gates, w_g, w_u, w_d):
    hit, picked, rank, gate = routing(ids, gates)
    code = jnp.where(picked, rank, -1.0).T.reshape(N_DEV, N_LOC, TOK)
    match = code[:, :, None, :] == jnp.arange(CAP, dtype=F32)[None, None, :, None]
    slot_tok = jnp.sum(jnp.where(match, jnp.arange(TOK, dtype=jnp.int32), 0), axis=-1)
    send = jnp.take(x_loc, slot_tok.reshape(-1), axis=0, mode='clip').reshape(N_DEV, N_LOC, CAP, HID)
    recv = lax.all_to_all(send, EXPERT_AXES, 0, 0)
    h_gate = jnp.einsum('slch,lhf->slcf', recv, w_g, preferred_element_type=F32)
    h_up = jnp.einsum('slch,lhf->slcf', recv, w_u, preferred_element_type=F32)
    act = (jax.nn.silu(h_gate) * h_up).astype(BF16)
    out = jnp.einsum('slcf,lfh->slch', act, w_d, preferred_element_type=F32).astype(BF16)
    back = lax.all_to_all(out, EXPERT_AXES, 0, 0).reshape(N_EXP * CAP, HID)
    rank_j = jnp.sum(jnp.where(hit, rank[:, None, :], 0.0), axis=-1).astype(jnp.int32)
    got = jnp.take(back, (ids * CAP + rank_j).reshape(-1), axis=0, mode='clip').reshape(TOK, -1, HID)
    return (x_loc.astype(F32) + jnp.sum(gates[:, :, None] * got, axis=1)).astype(BF16)


def solution(mesh):
    def local_layer(x, ids, gates, w1, w3, w2):
        codes, comb = tables(ids, gates)
        y, flag = moe(x, codes, comb, w1, w3, w2)
        return lax.cond(flag[0, 0] > 0.0, lambda: plain(x, ids, gates, w1, w3, w2), lambda: y)

    tok = P(TOKEN_AXES, None)
    w = P(EXPERT_AXES, None, None)
    return jax.shard_map(local_layer, mesh=mesh, in_specs=(tok, tok, tok, w, w, w), out_specs=tok, check_vma=False)
```

time: 1020 us -> 366 us (0.36)
  waiting for transfers between devices: 386 us -> 0 us
  Pallas kernels: 0 us -> 352 us
  blocking collectives: 285 us -> 0 us
  matrix products: 147 us -> 0.29 us
  local copies, waits for them, and re-layouts: 125 us -> 5.66 us
  other arithmetic: 68.3 us -> 4.26 us
    all_to_all x1 -> x0, waiting for transfers between devices: 386 us -> none  [local_layer(): back_buf = lax.all_to_all(exp_out, EXPERT_AXES, 0, 0)]
    pallas_call x0 -> x1, Pallas kernels: none -> 352 us  [moe(): pl.pallas_call(moe_kernel, out_shape=(jax.ShapeDtypeStruct((TOK, HID), BF...]
    all_to_all x1 -> x0, blocking collectives: 285 us -> none  [local_layer(): recv_buf = lax.all_to_all(send_buf, EXPERT_AXES, 0, 0)]
    dot_general x3 -> x1, matrix products: 147 us -> 0.29 us  [routing(): rank = jnp.dot(below, picked.astype(BF16), preferred_element_type=F32)]
    gather x3 -> x0, local copies, waits for them, and re-layouts: 86.7 us -> none  [the longest x2 55.7 us: local_layer(): jnp.take(back_flat, slot_idx, axis=0).reshape(tok_dev, top_k, hid_dim)]
    another operation x3 -> x0, other arithmetic: 32.4 us -> none
    convert_element_type x1 -> x0, local copies, waits for them, and re-layouts: 21 us -> none  [local_layer(): jnp.einsum('slcf,lfh->slch', act_bf, w_d, preferred_element_type=jnp.floa...]
    reduce_sum x2 -> x4, other arithmetic: 19.6 us -> 1.15 us  [the longest x1 0.83 us: routing(): gate = jnp.sum(jnp.where(hit, gates[:, :, None], 0.0), axis=1)]
  transfers between devices with their start and end apart: 1 -> 0, of which waited for: 1 -> 0; matrix products, arithmetic and copies ran while one was open for 0% -> 0% of each run, Pallas kernels for 0% -> 0%
where the time goes in v2:
time: 366 us; the launch traced here: 364 us
  Pallas kernels  352 us (96%)
  local copies, waits for them, and re-layouts  5.66 us (2%)
  other arithmetic  4.26 us (1%)
    pallas_call x1, Pallas kernels, moe(): pl.pallas_call(moe_kernel, out_shape=(jax.ShapeDtypeStruct((TOK, HID), BF...  352 us

profile of v2, /device:TPU:5, one launch (start us, length us, event | category | flops | bytes accessed | tf_op | source)
XLA Modules:
  0.0 363.9 jit_solution(10069440621698226401)
XLA Ops:
  0.0 0.8 fusion.19
  0.8 0.1 convert_reduce_fusion
  0.9 0.1 lt.37
  1.0 0.1 copy.45
  1.1 0.1 multiply_reduce_fusion.1
  1.2 0.1 copy.46
  1.3 0.1 add.45
  1.4 0.1 copy.42
  1.5 0.3 add_select_fusion
  1.8 0.1 copy.44
  2.0 0.1 add.42
  2.1 0.1 add.43
  2.3 0.1 lt.39
  2.4 0.1 lt.35
  2.6 0.1 reduce_sum.65
  2.7 0.6 reduce_max.9
  4.0 0.8 fusion.20.codes_ref
  4.8 0.8 select_reduce_fusion.2
  5.6 0.1 copy.50
  5.8 0.8 pad_maximum_fusion.comb_ref
  6.6 352.1 %moe.1 = (bf16[512,2048]{1,0:T(8,128)(2,1)}, f32[8,128]{1,0:T(8,128)}, bf16[16,512,2048]{2,1,0:T(8,128)(2,1)}, bf16[16,240,2048]{2,1,0:T(8,128)(2,1)}, bf16[16,240,2048]{2,1,0:T(8,128)(2,1)}) custom-call(bf16[512,2048]{1,0:T(8,128)(2,1)} %x_ref.1, f32[16,8,512]{2,1,0:T(8,128)} %fusion.20.codes_ref, f32[512,128]{1,0:T(8,128)} %pad_maximum_fusion.comb_ref, ...), custom_call_target="tpu_custom_call" | custom-call | tf_op jit(solution)/shard_map/moe/pallas_call | solution.py:352
  358.7 1.2 slice.3
  360.5 0.2 conditional.1
  360.8 3.2 copy.64
  (7 shorter events, 0.2 us)

commit v3 on v2

--- a/solution.py
+++ b/solution.py
@@ -59,9 +59,9 @@
 
 
 def moe_kernel(x_ref, codes_ref, comb_ref, w1_ref, w3_ref, w2_ref,
-               y_ref, flag_ref, x_all, h_send, h_recv,
+               y_ref, flag_ref, x_all, h_send, h_recv, h_pass,
                wb1, wb3, wb2, rows, act, xb, sb, meta, acc,
-               w_sem, xl_sem, xs_sem, xr_sem, ms_sem, mr_sem, sl_sem, rs_sem, rr_sem, rl_sem):
+               w_sem, xl_sem, xs_sem, xr_sem, ms_sem, mr_sem, sl_sem, rs_sem, rr_sem, rl_sem, ps_sem, pr_sem):
     ez, ey, ex = (lax.axis_index(a) for a in TOKEN_AXES)
     core, xc = ex % 2, ex // 2
     my_tok = (ez * 2 + ey) * 4 + ex
@@ -69,12 +69,15 @@
 
     def place(q, other):
         cs = core + other * (1 - 2 * core)
+        return moved(q, cs, cs)
+
+    def moved(q, cs, to_core):
         fa, fb, fc = flips(q)
         fx = fa * (1 - cs) + fb * cs
         fy = fb * (1 - cs) + fc * cs
         fz = fc * (1 - cs) + fa * cs
         pz, py, px = ez + fz * (1 - 2 * ez), ey + fy * (1 - 2 * ey), xc + fx * (1 - 2 * xc)
-        return pz, py, 2 * px + cs
+        return pz, py, 2 * px + to_core
 
     def tok_num(p):
         return (p[0] * 2 + p[1]) * 4 + p[2]
@@ -208,6 +211,19 @@
             src_ref=h_send.at[d], dst_ref=h_recv.at[my_exp], send_sem=rs_sem.at[d],
             recv_sem=rr_sem.at[my_exp], device_id=dev, device_id_type=MESH)
 
+    def via_copy(k):
+        i, c2 = k // 2, k % 2
+        return pltpu.make_async_remote_copy(
+            src_ref=h_send.at[2 * FIRST[2] + k], dst_ref=h_pass.at[k], send_sem=rs_sem.at[2 * FIRST[2] + k],
+            recv_sem=pr_sem.at[k], device_id=place((i + 1) % 3 + 1, c2), device_id_type=MESH)
+
+    def pass_on(k):
+        i, c2 = k // 2, k % 2
+        num = exp_num(moved((i + 1) % 3 + 1, core, core + c2 * (1 - 2 * core)))
+        return pltpu.make_async_remote_copy(
+            src_ref=h_pass.at[k], dst_ref=h_recv.at[num], send_sem=ps_sem.at[k],
+            recv_sem=rr_sem.at[num], device_id=place((i + 2) % 3 + 1, 0), device_id_type=MESH)
+
     def stage(d):
         return pltpu.make_async_copy(sb.at[d % 2], h_send.at[d], sl_sem.at[d % 2])
 
@@ -234,14 +250,17 @@
             @pl.when(k > 0)
             def _():
                 stage(d - 1).wait()
-                if ci == 0:
-                    pass
-                else:
+                if ci == 1:
                     ret_copy(d - 1).start()
+                elif ci == 2:
+                    via_copy(k - 1).start()
 
         last = d0 + n - 1
         stage(last).wait()
-        ret_copy(last).start()
+        if ci == 2:
+            via_copy(n - 1).start()
+        elif ci < 2:
+            ret_copy(last).start()
 
     def experts(ci, between=None):
         @pl.loop(0, N_LOC)
@@ -301,8 +320,22 @@
 
     pltpu.make_async_copy(h_send.at[0], sb.at[0], rl_sem.at[0]).start()
 
+    def hand_on(first):
+        @pl.loop(0, 3)
+        def _(i):
+            via_copy(2 * i + first).wait_recv()
+            pass_on(2 * i + first).start()
+
+    def far():
+        hand_on(1)
+        for d in (14, 15):
+            ret_copy(d).start()
+
     @pl.loop(0, N_DEV)
     def _(d):
+        pl.when(d == 3)(lambda: hand_on(0))
+        pl.when(d == 6)(far)
+
         @pl.when(d + 1 < N_DEV)
         def _():
             came(d + 1)
@@ -337,6 +370,10 @@
         meta_copy(d).wait_send()
         ret_copy(d).wait_send()
 
+    @pl.loop(0, 6)
+    def _(k):
+        pass_on(k).wait_send()
+
 
 def x_to_f32(x_ref, xb, xl_sem, acc):
     c = pltpu.make_async_copy(x_ref, xb.at[0], xl_sem.at[0])
@@ -357,9 +394,10 @@
             jax.ShapeDtypeStruct((N_DEV, TOK, HID), BF16),
             jax.ShapeDtypeStruct((N_DEV, RET, HID), BF16),
             jax.ShapeDtypeStruct((N_DEV, RET, HID), BF16),
+            jax.ShapeDtypeStruct((6, RET, HID), BF16),
         ),
         in_specs=[hbm, hbm, vmem, hbm, hbm, hbm],
-        out_specs=(vmem, vmem, hbm, hbm, hbm),
+        out_specs=(vmem, vmem, hbm, hbm, hbm, hbm),
         scratch_shapes=[
             pltpu.VMEM((2, HID, FFN), BF16),
             pltpu.VMEM((2, HID, FFN), BF16),
@@ -371,7 +409,7 @@
             pltpu.VMEM((N_DEV, 8, TOK), F32),
             pltpu.VMEM((TOK, HID), F32),
             dma((2, 3)), dma((2,)), dma((15,)), dma((16,)), dma((16,)), dma((16,)),
-            dma((2,)), dma((16,)), dma((16,)), dma((2,)),
+            dma((2,)), dma((16,)), dma((16,)), dma((2,)), dma((6,)), dma((6,)),
         ],
         compiler_params=pltpu.CompilerParams(
             collective_id=0, has_side_effects=True, vmem_limit_bytes=67_043_328),
@@ -382,19 +420,28 @@
 
 def plain(x_loc, ids, gates, w_g, w_u, w_d):
     hit, picked, rank, gate = routing(ids, gates)
-    code = jnp.where(picked, rank, -1.0).T.reshape(N_DEV, N_LOC, TOK)
-    match = code[:, :, None, :] == jnp.arange(CAP, dtype=F32)[None, None, :, None]
-    slot_tok = jnp.sum(jnp.where(match, jnp.arange(TOK, dtype=jnp.int32), 0), axis=-1)
-    send = jnp.take(x_loc, slot_tok.reshape(-1), axis=0, mode='clip').reshape(N_DEV, N_LOC, CAP, HID)
+    code = jnp.where(picked, rank, -1.0)
+    match = code.T.reshape(N_DEV, N_LOC, 1, TOK) == jnp.arange(CAP, dtype=F32)[None, None, :, None]
+    send = jnp.einsum('slct,th->slch', match.astype(BF16), x_loc, preferred_element_type=F32).astype(BF16)
     recv = lax.all_to_all(send, EXPERT_AXES, 0, 0)
-    h_gate = jnp.einsum('slch,lhf->slcf', recv, w_g, preferred_element_type=F32)
-    h_up = jnp.einsum('slch,lhf->slcf', recv, w_u, preferred_element_type=F32)
-    act = (jax.nn.silu(h_gate) * h_up).astype(BF16)
-    out = jnp.einsum('slcf,lfh->slch', act, w_d, preferred_element_type=F32).astype(BF16)
-    back = lax.all_to_all(out, EXPERT_AXES, 0, 0).reshape(N_EXP * CAP, HID)
-    rank_j = jnp.sum(jnp.where(hit, rank[:, None, :], 0.0), axis=-1).astype(jnp.int32)
-    got = jnp.take(back, (ids * CAP + rank_j).reshape(-1), axis=0, mode='clip').reshape(TOK, -1, HID)
-    return (x_loc.astype(F32) + jnp.sum(gates[:, :, None] * got, axis=1)).astype(BF16)
+
+    def expert(args):
+        rows, one, three, two = args
+        h_gate = jnp.dot(rows, one, preferred_element_type=F32)
+        h_up = jnp.dot(rows, three, preferred_element_type=F32)
+        act = (jax.nn.silu(h_gate) * h_up).astype(BF16)
+        return jnp.dot(act, two, preferred_element_type=F32).astype(BF16)
+
+    out = lax.map(expert, (recv.transpose(1, 0, 2, 3).reshape(N_LOC, N_DEV * CAP, HID), w_g, w_u, w_d))
+    back = lax.all_to_all(out.reshape(N_LOC, N_DEV, CAP, HID).transpose(1, 0, 2, 3), EXPERT_AXES, 0, 0)
+
+    def add(acc, args):
+        rows, code_e, gate_e = args
+        share = jnp.where(code_e[:, None] == jnp.arange(CAP, dtype=F32)[None, :], gate_e[:, None], 0.0)
+        return acc + jnp.dot(share, rows.astype(F32), precision=lax.Precision.HIGHEST), None
+
+    total = lax.scan(add, x_loc.astype(F32), (back.reshape(N_EXP, CAP, HID), code.T, gate.T))[0]
+    return total.astype(BF16)
 
 
 def solution(mesh):

time: 366 us -> 363 us (level)
  the two profiles are of different devices: /device:TPU:5 before, /device:TPU:1 now
where the time goes in v3:
time: 363 us
  Pallas kernels  351 us (97%)
  local copies, waits for them, and re-layouts  5.67 us (2%)
  other arithmetic  4.26 us (1%)
    pallas_call x1, Pallas kernels, moe(): pl.pallas_call(moe_kernel, out_shape=(jax.ShapeDtypeStruct((TOK, HID), BF...  351 us

profile of v3, /device:TPU:1, one launch (start us, length us, event | category | flops | bytes accessed | tf_op | source)
XLA Modules:
  0.0 362.6 jit_solution(16121704581453125058)
XLA Ops:
  0.0 0.8 fusion.37
  0.8 0.1 convert_reduce_fusion
  0.9 0.1 lt.43
  1.0 0.1 copy.31
  1.1 0.1 multiply_reduce_fusion
  1.2 0.1 copy.32
  1.3 0.1 add.48
  1.4 0.1 copy.28
  1.5 0.3 add_select_fusion
  1.8 0.1 copy.30
  2.0 0.1 add.45
  2.1 0.1 add.46
  2.3 0.1 lt.45
  2.4 0.1 lt.41
  2.6 0.1 reduce_sum.47
  2.7 0.6 reduce_max.9
  4.0 0.8 fusion.38.codes_ref
  4.8 0.8 select_reduce_fusion.1
  5.6 0.1 copy.36
  5.8 0.8 pad_maximum_fusion.comb_ref
  6.6 350.7 %moe.1 = (bf16[512,2048]{1,0:T(8,128)(2,1)}, f32[8,128]{1,0:T(8,128)}, bf16[16,512,2048]{2,1,0:T(8,128)(2,1)}, bf16[16,240,2048]{2,1,0:T(8,128)(2,1)}, bf16[16,2...) custom-call(bf16[512,2048]{1,0:T(8,128)(2,1)} %x_ref.1, f32[16,8,512]{2,1,0:T(8,128)} %fusion.38.codes_ref, ...), custom_call_target="tpu_custom_call" | custom-call | tf_op jit(solution)/shard_map/moe/pallas_call | solution.py:389
  357.4 1.2 slice.3
  359.2 0.2 conditional.1
  359.4 3.2 copy.60
  (7 shorter events, 0.2 us)
